TPU v7x, 32 devices: a whole 2x2x4 slice. The times are simulated.
32 devices in a mesh: rows: 16 (over z, y, x), feat: 2 (over core).
Axes of the slice: x: 2, y: 2, z: 4, core: 2. Of those that a mesh axis runs over, the one named last changes fastest.
Arguments:
- queries: bfloat16 [1024, 128], P('rows', 'feat'), may hold values from -6 to 6
- corpus: bfloat16 [524288, 128], P(('rows', 'feat')), as said below
- candidates: int32 [1024, 100], P(('rows', 'feat')), may hold values from 0 to 524287, as said below
- threshold: int32 [1024], replicated, may hold values from 100 to 199, as said below
Outputs:
- exceed: float32 [1024], P(('rows', 'feat'))
- candidate_scores: float32 [1024, 100], P(('rows', 'feat'))
Inputs may be any that keep to these rules, and one draw needn't show every extreme that they name: Passage ids. Of the 3200 candidates of one device's queries (aligned blocks of 32 rows), at most 100 lie in the 16384 passages of any one device, and exactly 100 in some device's. `corpus`: passage embeddings of order one or smaller; their scale differs between passages. Some query has threshold 100 and some 199.
All inputs are finite; a program needn't handle non-finite values.
Results may differ from a plain program's by a relative error of at most 0.00035.
Values may be sent and summed in bfloat16 or wider, within the bound.
A program may use at most 64 MiB of HBM per device.

v0:
```python
import jax
import jax.numpy as jnp
from jax import lax
from jax.sharding import PartitionSpec as P


def body(queries, corpus, candidates, threshold):
    rows_dev = corpus.shape[0]
    width = corpus.shape[1]
    shards = lax.axis_size("rows") * lax.axis_size("feat")
    owned_queries = candidates.shape[0]
    per_query = candidates.shape[1]
    npass_all = rows_dev * shards
    cutoff = threshold.astype(jnp.float32) * 0.01
    owner = lax.axis_index(("rows", "feat"))
    full_rows = lax.all_gather(queries, "feat", axis=1, tiled=True)
    whole = lax.all_gather(full_rows, "rows", axis=0, tiled=True)
    query_count = whole.shape[0]
    block = 2048
    corpus_blocks = corpus.reshape(rows_dev // block, block, width)

    def visit(total, block_rows):
        scores = lax.dot_general(
            whole, block_rows, (((1,), (1,)), ((), ())), preferred_element_type=jnp.float32
        )
        return (total + jnp.sum(jnp.maximum(scores - cutoff[:, None], 0.0), axis=1), None)

    total, _ = lax.scan(visit, jnp.zeros((query_count,), jnp.float32), corpus_blocks)
    flat_ids = candidates.reshape(-1)
    total_ids = flat_ids.shape[0]
    capacity = (total_ids + shards - 1) // shards
    target = flat_ids // rows_dev
    onehot = (target[:, None] == jnp.arange(shards, dtype=jnp.int32)[None, :]).astype(jnp.int32)
    before = jnp.cumsum(onehot, axis=0) - onehot
    rank = jnp.sum(before * onehot, axis=1)
    query_ids = owner * owned_queries + jnp.arange(total_ids, dtype=jnp.int32) // per_query
    fields = jnp.stack([flat_ids - target * rows_dev, query_ids], axis=1)
    send_both = jnp.zeros((shards, capacity, 2), jnp.int32).at[target, rank].set(fields)
    n_rows = lax.axis_size("rows")
    n_feat = lax.axis_size("feat")
    received = lax.all_to_all(
        lax.all_to_all(
            send_both.reshape(n_rows, n_feat, capacity * 2),
            "rows",
            split_axis=0,
            concat_axis=0,
            tiled=True,
        ),
        "feat",
        split_axis=1,
        concat_axis=1,
        tiled=True,
    )
    received = received.reshape(shards * capacity, 2)
    picked = corpus[received[:, 0]]
    asked = whole[received[:, 1]]
    values = jnp.einsum("kd,kd->k", picked, asked, preferred_element_type=jnp.float32).reshape(
        n_rows, n_feat, capacity
    )
    partials = total.reshape(n_rows, n_feat, owned_queries)
    answers, mass_parts = (
        lax.all_to_all(
            lax.all_to_all(values, "rows", split_axis=0, concat_axis=0, tiled=True),
            "feat",
            split_axis=1,
            concat_axis=1,
            tiled=True,
        ),
        lax.all_to_all(
            lax.all_to_all(partials, "rows", split_axis=0, concat_axis=0, tiled=True),
            "feat",
            split_axis=1,
            concat_axis=1,
            tiled=True,
        ),
    )
    exceed = jnp.sum(mass_parts, axis=(0, 1)) * (8.0 / npass_all)
    candidate_scores = answers.reshape(shards, capacity)[target, rank].reshape(
        owned_queries, per_query
    )
    return (exceed, candidate_scores)


def solution(mesh):
    return jax.shard_map(
        body,
        mesh=mesh,
        in_specs=(P("rows", "feat"), P(("rows", "feat"), None), P(("rows", "feat"), None), P()),
        out_specs=(P(("rows", "feat")), P(("rows", "feat"), None)),
        check_vma=False,
    )
```

profile of v0, /device:TPU:0, one launch (start us, length us, event | category | flops | bytes accessed | tf_op | source)
XLA Modules:
  0.0 177.3 jit_solution(1144586767254924828)
XLA Ops:
  0.6 0.8 copy.40
  1.4 2.0 %all_gather.6 = bf16[64,128]{0,1:T(8,128)(2,1)S(1)} all-gather(bf16[64,64]{0,1:T(8,128)(2,1)S(1)} %copy.40), channel_id=1, replica_groups=mesh['rows'=16,'feat'=2] {'feat'}, dimensions={1}, use_global_device_ids=true | all-gather | bytes 24576 | tf_op jit(solution)/shard_map/all_gather | solution.py:16
  3.4 0.1 copy.41
  3.5 43.7 %all_gather.7 = bf16[1024,128]{1,0:T(8,128)(2,1)S(1)} all-gather(bf16[64,128]{1,0:T(8,128)(2,1)S(1)} %copy.41), channel_id=1, replica_groups=mesh['rows'=16,'feat'=2] {'rows'}, dimensions={0}, use_global_device_ids=true | all-gather | bytes 278528 | tf_op jit(solution)/shard_map/all_gather | solution.py:17
  47.2 0.7 convert_multiply_fusion.1
  47.9 18.8 %while.11 = (s32[]{:T(128)}, f32[1024]{0:T(1024)S(1)}, bf16[8,2048,128]{2,1,0:T(8,128)(2,1)}, bf16[1024,128]{1,0:T(8,128)(2,1)S(1)}, f32[1024]{0:T(1024)S(1)}, /*index=5*/s32[]{:T(128)}, s32[]{:T(128)}) while((s32[]{:T(128)}, f32[1024]{0:T(1024)S(1)}, bf16[8,2048,128]{2,1,0:T(8,128)(2,1)}, bf16[1024,128]{1,0:T(8,128)(2,1)S(1)}, ...), condition=%wide.region_2.3_spmd.clone, body=%wide.region_0.2_spmd.clone.sunk | while | flops 543163392 | bytes 807511 | solution.py:28
  47.9 2.3 %maximum_reduce_fusion.2 = f32[1024]{0:T(1024)S(1)} fusion(bf16[1024,128]{1,0:T(8,128)(2,1)S(1)} %get-tuple-element.115, f32[1024]{0:T(1024)S(1)} %get-tuple-element.116, bf16[8,2048,128]{2,1,0:T(8,128)(2,1)} %get-tuple-element.114, s32[]{:T(128)} %get-tuple-element.105), kind=kOutput, calls=%fused_computation.4.clone.1 | convolution fusion | flops 543161344 | bytes 795136 | tf_op jit(solution)/shard_map/while/body/eval_jaxpr/dot_general | solution.py:23
  50.2 2.3 %maximum_reduce_fusion.2 = f32[1024]{0:T(1024)S(1)} fusion(bf16[1024,128]{1,0:T(8,128)(2,1)S(1)} %get-tuple-element.115, f32[1024]{0:T(1024)S(1)} %get-tuple-element.116, bf16[8,2048,128]{2,1,0:T(8,128)(2,1)} %get-tuple-element.114, s32[]{:T(128)} %get-tuple-element.105), kind=kOutput, calls=%fused_computation.4.clone.1 | convolution fusion | flops 543161344 | bytes 795136 | tf_op jit(solution)/shard_map/while/body/eval_jaxpr/dot_general | solution.py:23
  52.6 2.3 %maximum_reduce_fusion.2 = f32[1024]{0:T(1024)S(1)} fusion(bf16[1024,128]{1,0:T(8,128)(2,1)S(1)} %get-tuple-element.115, f32[1024]{0:T(1024)S(1)} %get-tuple-element.116, bf16[8,2048,128]{2,1,0:T(8,128)(2,1)} %get-tuple-element.114, s32[]{:T(128)} %get-tuple-element.105), kind=kOutput, calls=%fused_computation.4.clone.1 | convolution fusion | flops 543161344 | bytes 795136 | tf_op jit(solution)/shard_map/while/body/eval_jaxpr/dot_general | solution.py:23
  54.9 2.3 %maximum_reduce_fusion.2 = f32[1024]{0:T(1024)S(1)} fusion(bf16[1024,128]{1,0:T(8,128)(2,1)S(1)} %get-tuple-element.115, f32[1024]{0:T(1024)S(1)} %get-tuple-element.116, bf16[8,2048,128]{2,1,0:T(8,128)(2,1)} %get-tuple-element.114, s32[]{:T(128)} %get-tuple-element.105), kind=kOutput, calls=%fused_computation.4.clone.1 | convolution fusion | flops 543161344 | bytes 795136 | tf_op jit(solution)/shard_map/while/body/eval_jaxpr/dot_general | solution.py:23
  57.3 2.3 %maximum_reduce_fusion.2 = f32[1024]{0:T(1024)S(1)} fusion(bf16[1024,128]{1,0:T(8,128)(2,1)S(1)} %get-tuple-element.115, f32[1024]{0:T(1024)S(1)} %get-tuple-element.116, bf16[8,2048,128]{2,1,0:T(8,128)(2,1)} %get-tuple-element.114, s32[]{:T(128)} %get-tuple-element.105), kind=kOutput, calls=%fused_computation.4.clone.1 | convolution fusion | flops 543161344 | bytes 795136 | tf_op jit(solution)/shard_map/while/body/eval_jaxpr/dot_general | solution.py:23
  59.6 2.3 %maximum_reduce_fusion.2 = f32[1024]{0:T(1024)S(1)} fusion(bf16[1024,128]{1,0:T(8,128)(2,1)S(1)} %get-tuple-element.115, f32[1024]{0:T(1024)S(1)} %get-tuple-element.116, bf16[8,2048,128]{2,1,0:T(8,128)(2,1)} %get-tuple-element.114, s32[]{:T(128)} %get-tuple-element.105), kind=kOutput, calls=%fused_computation.4.clone.1 | convolution fusion | flops 543161344 | bytes 795136 | tf_op jit(solution)/shard_map/while/body/eval_jaxpr/dot_general | solution.py:23
  62.0 2.3 %maximum_reduce_fusion.2 = f32[1024]{0:T(1024)S(1)} fusion(bf16[1024,128]{1,0:T(8,128)(2,1)S(1)} %get-tuple-element.115, f32[1024]{0:T(1024)S(1)} %get-tuple-element.116, bf16[8,2048,128]{2,1,0:T(8,128)(2,1)} %get-tuple-element.114, s32[]{:T(128)} %get-tuple-element.105), kind=kOutput, calls=%fused_computation.4.clone.1 | convolution fusion | flops 543161344 | bytes 795136 | tf_op jit(solution)/shard_map/while/body/eval_jaxpr/dot_general | solution.py:23
  64.3 2.3 %maximum_reduce_fusion.2 = f32[1024]{0:T(1024)S(1)} fusion(bf16[1024,128]{1,0:T(8,128)(2,1)S(1)} %get-tuple-element.115, f32[1024]{0:T(1024)S(1)} %get-tuple-element.116, bf16[8,2048,128]{2,1,0:T(8,128)(2,1)} %get-tuple-element.114, s32[]{:T(128)} %get-tuple-element.105), kind=kOutput, calls=%fused_computation.4.clone.1 | convolution fusion | flops 543161344 | bytes 795136 | tf_op jit(solution)/shard_map/while/body/eval_jaxpr/dot_general | solution.py:23
  66.7 0.7 reshape.217
  67.3 4.1 %all-to-all-start = ((f32[16,2,32]{2,1,0:T(2,128)}), f32[16,2,32]{2,1,0:T(2,128)}, u32[]{:S(2)}, u32[]{:S(2)}) async-start(f32[16,2,32]{2,1,0:T(2,128)} %reshape.217), calls=%async_computation | async-start | bytes 32768 | tf_op jit(solution)/shard_map/all_to_all | solution.py:70
  71.5 0.0 copy-done
  71.5 0.1 reshape.220
  71.6 0.1 reshape.219
  71.7 0.1 reshape.218
  71.8 0.1 fusion.6
  71.9 0.0 copy-start.2
  71.9 0.0 copy-start.1
  71.9 9.2 %reduce-window.6 = s32[32,25,128]{2,1,0:T(8,128)S(1)} reduce-window(s32[32,25,128]{2,1,0:T(8,128)S(1)} %fusion.6, s32[]{:T(128)} %constant.28.clone.1), window={size=1x1x128 pad=0_0x0_0x127_0}, to_apply=%region_4.5 | reduce-window | flops 13004800 | bytes 819204 | tf_op jit(solution)/shard_map/reduce-window
  81.1 0.8 slice_reduce_fusion
  81.9 0.2 reduce-window.9
  82.1 0.2 broadcast_add_fusion
  82.3 0.3 fusion.9
  82.6 0.1 or_reduce_fusion
  82.9 0.0 copy-done.2
  82.9 0.1 and_reduce_fusion
  83.0 0.1 pad_add_fusion.1
  83.1 0.6 broadcast_select_fusion
  83.7 0.5 copy.44
  84.2 13.8 %scatter_custom_fusion = s32[3200,2]{1,0:T(8,128)S(1)} fusion(s32[3200]{0:T(1024)} %broadcast_select_fusion, s32[3200,2]{1,0:T(8,128)S(1)} %copy.44, s32[]{:T(128)} %constant.28.clone.1), kind=kCustom, calls=%fused_computation.11 | custom fusion | bytes 26112
  98.1 1.3 reshape.222
  99.4 0.0 all-to-all-done
  99.4 0.7 copy.66
  100.1 0.1 reshape.269
  100.2 3.7 %all_to_all.30 = f32[2,1,512]{2,1,0:T(1,128)S(1)} all-to-all(f32[2,1,512]{2,1,0:T(1,128)S(1)} %reshape.269), channel_id=1, replica_groups=mesh['rows'=16,'feat'=2] {'feat'}, dimensions={0} | all-to-all | bytes 8192 | tf_op jit(solution)/shard_map/all_to_all | solution.py:69
  103.8 6.8 %all-to-all-start.2 = ((s32[16,2,200]{2,1,0:T(2,128)}), s32[16,2,200]{2,1,0:T(2,128)S(1)}, u32[]{:S(2)}, u32[]{:S(2)}) async-start(s32[16,2,200]{2,1,0:T(2,128)} %reshape.222), calls=%async_computation.2 | async-start | bytes 65536 | tf_op jit(solution)/shard_map/all_to_all | solution.py:42
  110.7 0.5 broadcast.292
  111.2 0.7 reduce.15
  111.8 0.1 reshape.270
  111.9 0.5 bitcast_reduce_fusion
  112.5 5.6 %all-to-all-done.2 = s32[16,2,200]{2,1,0:T(2,128)S(1)} async-done(((s32[16,2,200]{2,1,0:T(2,128)}), s32[16,2,200]{2,1,0:T(2,128)S(1)}, u32[]{:S(2)}, u32[]{:S(2)}) %all-to-all-start.2) | async-done | bytes 25632 | tf_op jit(solution)/shard_map/all_to_all | solution.py:42
  118.1 3.7 %all_to_all.31 = s32[16,2,200]{2,0,1:T(8,128)S(1)} all-to-all(s32[16,2,200]{2,0,1:T(8,128)S(1)} %copy.45), channel_id=1, replica_groups=mesh['rows'=16,'feat'=2] {'feat'}, dimensions={1} | all-to-all | bytes 51200 | tf_op jit(solution)/shard_map/all_to_all | solution.py:41
  121.8 0.5 reshape.223
  122.3 1.7 fusion.17
  124.0 1.9 %copy.57 = s32[3200,1]{0,1:T(1,128)S(1)} copy(s32[3200,1]{1,0:T(8,128)} %get-tuple-element.61) | data formatting | bytes 25600
  126.0 0.1 fusion.15
  126.0 6.7 %gather_fusion.1 = bf16[3200,128]{1,0:T(8,128)(2,1)S(1)} fusion(bf16[1024,128]{1,0:T(8,128)(2,1)S(1)} %get-tuple-element.119, s32[4096]{0:T(1024)S(1)} %pad_clamp_fusion), kind=kCustom, calls=%fused_computation.1 | custom fusion | bytes 1651200 | tf_op jit(solution)/shard_map/gather | solution.py:56
  132.8 0.5 copy.56
  133.3 0.1 fusion.14
  133.3 8.5 %gather_fusion = bf16[3200,128]{1,0:T(8,128)(2,1)S(1)} fusion(bf16[16384,128]{1,0:T(8,128)(2,1)} %bitcast.35, s32[4096]{0:T(1024)S(1)} %pad_clamp_fusion.1), kind=kCustom, calls=%fused_computation | custom fusion | bytes 1651200 | tf_op jit(solution)/shard_map/gather | solution.py:55
  141.8 0.0 copy-start.3
  141.9 0.5 fusion.3
  142.4 0.7 reshape.224
  143.1 3.5 %all-to-all-start.4 = ((f32[16,2,100]{2,1,0:T(2,128)}), f32[16,2,100]{2,1,0:T(2,128)S(1)}, u32[]{:S(2)}, u32[]{:S(2)}) async-start(f32[16,2,100]{2,1,0:T(2,128)} %reshape.224), calls=%async_computation.4 | async-start | bytes 32768 | tf_op jit(solution)/shard_map/all_to_all | solution.py:63
  146.6 0.5 broadcast_multiply_fusion
  147.1 6.8 %all-to-all-done.4 = f32[16,2,100]{2,1,0:T(2,128)S(1)} async-done(((f32[16,2,100]{2,1,0:T(2,128)}), f32[16,2,100]{2,1,0:T(2,128)S(1)}, u32[]{:S(2)}, u32[]{:S(2)}) %all-to-all-start.4) | async-done | bytes 12832 | tf_op jit(solution)/shard_map/all_to_all | solution.py:63
  153.9 3.7 %all_to_all.32 = f32[16,2,100]{2,0,1:T(8,128)S(1)} all-to-all(f32[16,2,100]{2,0,1:T(8,128)S(1)} %copy.49), channel_id=1, replica_groups=mesh['rows'=16,'feat'=2] {'feat'}, dimensions={1} | all-to-all | bytes 25600 | tf_op jit(solution)/shard_map/all_to_all | solution.py:62
  157.6 19.0 %gather_fusion.2 = f32[3200]{0:T(1024)S(1)} fusion(f32[32,100]{1,0:T(8,128)S(1)} %bitcast.33, s32[3200]{0:T(1024)S(1)} %get-tuple-element.58), kind=kCustom, calls=%fused_computation.2 | custom fusion | bytes 51200 | tf_op jit(solution)/shard_map/gather | solution.py:78
  176.6 0.7 reshape.226
  (22 shorter events, 0.2 us)
Async XLA Ops:
  47.9 23.6 %copy-start = (s32[32,100]{1,0:T(8,128)S(1)}, s32[32,100]{1,0:T(8,128)}, u32[]{:S(2)}) copy-start(s32[32,100]{1,0:T(8,128)} %param.8) | copy-start | bytes 38404
  67.3 32.0 %all-to-all-start = ((f32[16,2,32]{2,1,0:T(2,128)}), f32[16,2,32]{2,1,0:T(2,128)}, u32[]{:S(2)}, u32[]{:S(2)}) async-start(f32[16,2,32]{2,1,0:T(2,128)} %reshape.217), calls=%async_computation | async-start | bytes 32768 | tf_op jit(solution)/shard_map/all_to_all | solution.py:70
  71.9 11.0 %copy-start.2 = (s32[2]{0:T(128)S(1)}, s32[2]{0:T(128)}, u32[]{:S(2)}) copy-start(s32[2]{0:T(128)} %constant.67) | copy-start | bytes 28
  71.9 11.1 %copy-start.1 = (s32[2]{0:T(128)S(1)}, s32[2]{0:T(128)}, u32[]{:S(2)}) copy-start(s32[2]{0:T(128)} %constant.64) | copy-start | bytes 28
  103.8 14.2 %all-to-all-start.2 = ((s32[16,2,200]{2,1,0:T(2,128)}), s32[16,2,200]{2,1,0:T(2,128)S(1)}, u32[]{:S(2)}, u32[]{:S(2)}) async-start(s32[16,2,200]{2,1,0:T(2,128)} %reshape.222), calls=%async_computation.2 | async-start | bytes 65536 | tf_op jit(solution)/shard_map/all_to_all | solution.py:42
  141.8 4.8 %copy-start.3 = (f32[32]{0:T(128)S(1)}, f32[32]{0:T(128)}, u32[]{:S(2)}) copy-start(f32[32]{0:T(128)} %bitcast_reduce_fusion) | copy-start | bytes 388
  143.1 10.8 %all-to-all-start.4 = ((f32[16,2,100]{2,1,0:T(2,128)}), f32[16,2,100]{2,1,0:T(2,128)S(1)}, u32[]{:S(2)}, u32[]{:S(2)}) async-start(f32[16,2,100]{2,1,0:T(2,128)} %reshape.224), calls=%async_computation.4 | async-start | bytes 32768 | tf_op jit(solution)/shard_map/all_to_all | solution.py:63
where the time goes:
time: 178 us; the launch traced here: 177 us
  local copies, waits for them, and re-layouts  59.9 us (34%)
  blocking collectives  56.8 us (32%)
  matrix products  18.5 us (10%)
  starting transfers between devices  14.4 us (8%)
  other arithmetic  14.1 us (8%)
  waiting for transfers between devices  12.4 us (7%)
    all_gather x1, blocking collectives, body(): whole = lax.all_gather(full_rows, 'rows', axis=0, tiled=True)  43.7 us
    gather x1, local copies, waits for them, and re-layouts, body(): answers.reshape(shards, capacity)[target, rank]  19 us
    dot_general x8, matrix products, visit(): lax.dot_general(whole, block_rows, (((1,), (1,)), ((), ())), preferred_el...  18.5 us
    unnamed x14, local copies, waits for them, and re-layouts  17.2 us
    another operation x3, other arithmetic  9.61 us
    gather x1, local copies, waits for them, and re-layouts, body(): picked = corpus[received[:, 0]]  8.49 us
    all_to_all x1, starting transfers between devices, body(): lax.all_to_all(send_both.reshape(n_rows, n_feat, capacity * 2), 'rows', s...  6.81 us
    all_to_all x1, waiting for transfers between devices, body(): lax.all_to_all(values, 'rows', split_axis=0, concat_axis=0, tiled=True)  6.78 us
  transfers between devices with their start and end apart: 3, of which 2 were waited for; matrix products, arithmetic and copies ran while one was open for 17% of the time, Pallas kernels for 0%

commit v1 on v0

--- a/solution.py
+++ b/solution.py
@@ -2,6 +2,27 @@
 import jax.numpy as jnp
 from jax import lax
 from jax.sharding import PartitionSpec as P
+
+
+def collect(value, axis, dim):
+    peers, index, span = (lax.axis_size(axis), lax.axis_index(axis), value.shape[dim])
+    ahead = [(i, (i + 1) % peers) for i in range(peers)]
+    downward = [(i, (i - 1) % peers) for i in range(peers)]
+    out = jnp.zeros((*value.shape[:dim], peers * span, *value.shape[dim + 1 :]), value.dtype)
+    out = lax.dynamic_update_slice_in_dim(out, value, index * span, axis=dim)
+    from_left = from_right = value
+    half = peers // 2
+    for hop in range(1, half + 1):
+        from_left = lax.ppermute(from_left, axis, ahead)
+        out = lax.dynamic_update_slice_in_dim(
+            out, from_left, (index - hop) % peers * span, axis=dim
+        )
+        if hop < peers - half:
+            from_right = lax.ppermute(from_right, axis, downward)
+            out = lax.dynamic_update_slice_in_dim(
+                out, from_right, (index + hop) % peers * span, axis=dim
+            )
+    return out
 
 
 def body(queries, corpus, candidates, threshold):
@@ -14,7 +35,7 @@
     cutoff = threshold.astype(jnp.float32) * 0.01
     owner = lax.axis_index(("rows", "feat"))
     full_rows = lax.all_gather(queries, "feat", axis=1, tiled=True)
-    whole = lax.all_gather(full_rows, "rows", axis=0, tiled=True)
+    whole = collect(full_rows, "rows", 0)
     query_count = whole.shape[0]
     block = 2048
     corpus_blocks = corpus.reshape(rows_dev // block, block, width)

time: 178 us -> 190 us (1.067)
  blocking collectives: 56.8 us -> 13.1 us
  starting transfers between devices: 14.4 us -> 51.1 us
  waiting for transfers between devices: 12.4 us -> 25 us
  local copies, waits for them, and re-layouts: 59.9 us -> 67 us
    all_gather x1 -> x0, blocking collectives: 43.7 us -> none  [body(): whole = lax.all_gather(full_rows, 'rows', axis=0, tiled=True)]
    ppermute x0 -> x15, starting transfers between devices: none -> 40.6 us  [the longest x7 35.9 us: collect(): from_right = lax.ppermute(from_right, axis, downward)]
    ppermute x0 -> x15, waiting for transfers between devices: none -> 13.4 us  [the longest x8 13.4 us: collect(): from_left = lax.ppermute(from_left, axis, ahead)]
    all_to_all x1, waiting for transfers between devices: 0.01 us -> 6.08 us  [body(): lax.all_to_all(partials, 'rows', split_axis=0, concat_axis=0, tiled=True)]
    all_to_all x1, waiting for transfers between devices: 5.6 us -> 0.01 us  [body(): lax.all_to_all(send_both.reshape(n_rows, n_feat, capacity * 2), 'rows', s...]
    dynamic_update_slice x0 -> x16, local copies, waits for them, and re-layouts: none -> 5.15 us  [the longest x8 2.21 us: collect(): lax.dynamic_update_slice_in_dim(out, from_left, (index - hop) % peers * s...]
    all_to_all x1, starting transfers between devices: 6.81 us -> 3.5 us  [body(): lax.all_to_all(send_both.reshape(n_rows, n_feat, capacity * 2), 'rows', s...]
    reshape x3, local copies, waits for them, and re-layouts: 0.31 us -> 2.46 us  [body(): flat_ids = candidates.reshape(-1)]
  transfers between devices with their start and end apart: 3 -> 18, of which waited for: 2 -> 8; matrix products, arithmetic and copies ran while one was open for 17% -> 27% of each run, Pallas kernels for 0% -> 0%
where the time goes in v1:
time: 190 us; the launch traced here: 189 us
  local copies, waits for them, and re-layouts  67 us (35%)
  starting transfers between devices  51.1 us (27%)
  waiting for transfers between devices  25 us (13%)
  matrix products  18.4 us (10%)
  blocking collectives  13.1 us (7%)
  other arithmetic  12.9 us (7%)
    ppermute x7, starting transfers between devices, collect(): from_right = lax.ppermute(from_right, axis, downward)  35.9 us
    gather x1, local copies, waits for them, and re-layouts, body(): answers.reshape(shards, capacity)[target, rank]  19 us
    dot_general x8, matrix products, visit(): lax.dot_general(whole, block_rows, (((1,), (1,)), ((), ())), preferred_el...  18.4 us
    unnamed x16, local copies, waits for them, and re-layouts  17.1 us
    ppermute x8, waiting for transfers between devices, collect(): from_left = lax.ppermute(from_left, axis, ahead)  13.4 us
    another operation x3, other arithmetic  9.61 us
    gather x1, local copies, waits for them, and re-layouts, body(): picked = corpus[received[:, 0]]  8.49 us
    gather x1, local copies, waits for them, and re-layouts, body(): asked = whole[received[:, 1]]  6.72 us
  transfers between devices with their start and end apart: 18, of which 8 were waited for; matrix products, arithmetic and copies ran while one was open for 27% of the time, Pallas kernels for 0%

profile of v1, /device:TPU:0, one launch (start us, length us, event | category | flops | bytes accessed | tf_op | source)
XLA Modules:
  0.0 188.9 jit_solution(9508828512468099624)
XLA Ops:
  0.6 0.8 copy.44
  1.4 2.0 %all_gather.3 = bf16[64,128]{0,1:T(8,128)(2,1)S(1)} all-gather(bf16[64,64]{0,1:T(8,128)(2,1)S(1)} %copy.44), channel_id=1, replica_groups=mesh['rows'=16,'feat'=2] {'feat'}, dimensions={1}, use_global_device_ids=true | all-gather | bytes 24576 | tf_op jit(solution)/shard_map/all_gather | solution.py:37
  3.4 0.7 copy.45
  4.1 2.8 %collective-permute-start = (bf16[64,128]{1,0:T(8,128)(2,1)}, bf16[64,128]{1,0:T(8,128)(2,1)}, u32[]{:S(2)}, u32[]{:S(2)}) collective-permute-start(bf16[64,128]{1,0:T(8,128)(2,1)} %copy.45), channel_id=1, source_target_pairs={{0,2},{2,4},{4,6},{6,8},{8,10},{10,12},{12,14},{14,16},{16,18},{18... | collective-permute-start | bytes 49160 | tf_op jit(solution)/shard_map/ppermute | solution.py:16
  6.9 4.0 %collective-permute-start.1 = (bf16[64,128]{1,0:T(8,128)(2,1)}, bf16[64,128]{1,0:T(8,128)(2,1)}, u32[]{:S(2)}, u32[]{:S(2)}) collective-permute-start(bf16[64,128]{1,0:T(8,128)(2,1)} %copy.45), channel_id=1, source_target_pairs={{0,30},{2,0},{4,2},{6,4},{8,6},{10,8},{12,10},{14,12},{16,14},{18,... | collective-permute-start | bytes 49160 | tf_op jit(solution)/shard_map/ppermute | solution.py:21
  10.9 0.8 reshape.220
  11.7 0.8 reshape.219
  12.6 0.8 reshape.218
  13.5 9.2 %reduce-window.6 = s32[32,25,128]{2,1,0:T(8,128)S(1)} reduce-window(s32[32,25,128]{2,1,0:T(8,128)S(1)} %fusion.6, s32[]{:T(128)} %constant.133.clone.1), window={size=1x1x128 pad=0_0x0_0x127_0}, to_apply=%region_4.5 | reduce-window | flops 13004800 | bytes 819204 | tf_op jit(solution)/shard_map/reduce-window
  22.8 0.8 slice_reduce_fusion
  24.7 0.5 copy.50
  25.3 13.7 %scatter_custom_fusion = s32[3200,2]{1,0:T(8,128)S(1)} fusion(s32[3200]{0:T(1024)S(1)} %broadcast_select_fusion, s32[3200,2]{1,0:T(8,128)S(1)} %copy.50, s32[]{:T(128)} %constant.133.clone.1), kind=kCustom, calls=%fused_computation.11 | custom fusion | bytes 25604
  39.0 1.3 reshape.222
  40.3 3.5 %all-to-all-start.2 = ((s32[16,2,200]{2,1,0:T(2,128)}), s32[16,2,200]{2,1,0:T(2,128)S(1)}, u32[]{:S(2)}, u32[]{:S(2)}) async-start(s32[16,2,200]{2,1,0:T(2,128)} %reshape.222), calls=%async_computation.2 | async-start | bytes 65536 | tf_op jit(solution)/shard_map/all_to_all | solution.py:63
  43.8 0.6 convert_multiply_fusion.1
  44.4 0.7 constant_dynamic-update-slice_fusion.15
  45.1 1.8 collective-permute-start.2
  47.0 3.8 %collective-permute-start.3 = (bf16[64,128]{1,0:T(8,128)(2,1)}, bf16[64,128]{1,0:T(8,128)(2,1)}, u32[]{:S(2)}, u32[]{:S(2)}) collective-permute-start(bf16[64,128]{1,0:T(8,128)(2,1)} %collective-permute-done.1), channel_id=1, source_target_pairs={{0,30},{2,0},{4,2},{6,4},{8,6},{10,8},{12,10},{14,12},{16,14},{18,... | collective-permute-start | bytes 49160 | tf_op jit(solution)/shard_map/ppermute | solution.py:21
  50.8 0.7 constant_dynamic-update-slice_fusion.14
  51.5 0.7 constant_dynamic-update-slice_fusion.13
  52.2 0.6 collective-permute-done.2
  52.8 5.6 %collective-permute-start.5 = (bf16[64,128]{1,0:T(8,128)(2,1)}, bf16[64,128]{1,0:T(8,128)(2,1)}, u32[]{:S(2)}, u32[]{:S(2)}) collective-permute-start(bf16[64,128]{1,0:T(8,128)(2,1)} %collective-permute-done.3), channel_id=1, source_target_pairs={{0,30},{2,0},{4,2},{6,4},{8,6},{10,8},{12,10},{14,12},{16,14},{18,... | collective-permute-start | bytes 49160 | tf_op jit(solution)/shard_map/ppermute | solution.py:21
  58.4 0.7 constant_dynamic-update-slice_fusion.12
  59.1 0.7 constant_dynamic-update-slice_fusion.11
  59.9 3.7 %all_to_all.30 = s32[16,2,200]{2,0,1:T(8,128)S(1)} all-to-all(s32[16,2,200]{2,0,1:T(8,128)S(1)} %copy.51), channel_id=1, replica_groups=mesh['rows'=16,'feat'=2] {'feat'}, dimensions={1} | all-to-all | bytes 51200 | tf_op jit(solution)/shard_map/all_to_all | solution.py:62
  63.6 0.5 reshape.223
  64.2 1.7 fusion.17
  65.9 1.9 %copy.63 = s32[3200,1]{0,1:T(1,128)S(1)} copy(s32[3200,1]{1,0:T(8,128)} %get-tuple-element.61) | data formatting | bytes 25600
  67.9 0.5 copy.62
  68.4 8.5 %gather_fusion = bf16[3200,128]{1,0:T(8,128)(2,1)S(1)} fusion(bf16[16384,128]{1,0:T(8,128)(2,1)} %param.7, s32[4096]{0:T(1024)S(1)} %pad_clamp_fusion.1), kind=kCustom, calls=%fused_computation | custom fusion | bytes 1651200 | tf_op jit(solution)/shard_map/gather | solution.py:76
  77.0 5.6 %collective-permute-start.7 = (bf16[64,128]{1,0:T(8,128)(2,1)}, bf16[64,128]{1,0:T(8,128)(2,1)S(1)}, u32[]{:S(2)}, u32[]{:S(2)}) collective-permute-start(bf16[64,128]{1,0:T(8,128)(2,1)} %collective-permute-done.5), channel_id=1, source_target_pairs={{0,30},{2,0},{4,2},{6,4},{8,6},{10,8},{12,10},{14,12},{16,14},{18,... | collective-permute-start | bytes 49160 | tf_op jit(solution)/shard_map/ppermute | solution.py:21
  82.6 0.7 constant_dynamic-update-slice_fusion.10
  83.3 0.7 constant_dynamic-update-slice_fusion.9
  84.5 5.6 %collective-permute-start.9 = (bf16[64,128]{1,0:T(8,128)(2,1)S(1)}, bf16[64,128]{1,0:T(8,128)(2,1)S(1)}, u32[]{:S(2)}, u32[]{:S(2)}) collective-permute-start(bf16[64,128]{1,0:T(8,128)(2,1)S(1)} %collective-permute-done.7), channel_id=1, source_target_pairs={{0,30},{2,0},{4,2},{6,4},{8,6},{10,8},{12,10},{14,12},{16,14},{18,... | collective-permute-start | bytes 49160 | tf_op jit(solution)/shard_map/ppermute | solution.py:21
  90.2 1.7 collective-permute-done.8
  91.9 5.6 %collective-permute-start.11 = (bf16[64,128]{1,0:T(8,128)(2,1)S(1)}, bf16[64,128]{1,0:T(8,128)(2,1)S(1)}, u32[]{:S(2)}, u32[]{:S(2)}) collective-permute-start(bf16[64,128]{1,0:T(8,128)(2,1)S(1)} %collective-permute-done.9), channel_id=1, source_target_pairs={{0,30},{2,0},{4,2},{6,4},{8,6},{10,8},{12,10},{14,12},{16,14},{18,... | collective-permute-start | bytes 49160 | tf_op jit(solution)/shard_map/ppermute | solution.py:21
  97.5 1.7 collective-permute-done.10
  99.2 5.6 %collective-permute-start.13 = (bf16[64,128]{1,0:T(8,128)(2,1)S(1)}, bf16[64,128]{1,0:T(8,128)(2,1)S(1)}, u32[]{:S(2)}, u32[]{:S(2)}) collective-permute-start(bf16[64,128]{1,0:T(8,128)(2,1)S(1)} %collective-permute-done.11), channel_id=1, source_target_pairs={{0,30},{2,0},{4,2},{6,4},{8,6},{10,8},{12,10},{14,12},{16,14},{18,... | collective-permute-start | bytes 49160 | tf_op jit(solution)/shard_map/ppermute | solution.py:21
  104.8 1.7 collective-permute-done.12
  106.6 7.3 %collective-permute-done.14 = bf16[64,128]{1,0:T(8,128)(2,1)S(1)} collective-permute-done((bf16[64,128]{1,0:T(8,128)(2,1)S(1)}, bf16[64,128]{1,0:T(8,128)(2,1)S(1)}, u32[]{:S(2)}, u32[]{:S(2)}) %collective-permute-start.14) | collective-permute-done | bytes 16416 | tf_op jit(solution)/shard_map/ppermute | solution.py:16
  113.9 6.7 %gather_fusion.1 = bf16[3200,128]{1,0:T(8,128)(2,1)S(1)} fusion(bf16[1024,128]{1,0:T(8,128)(2,1)S(1)} %constant_dynamic-update-slice_fusion, s32[4096]{0:T(1024)S(1)} %pad_clamp_fusion), kind=kCustom, calls=%fused_computation.1 | custom fusion | bytes 1651200 | tf_op jit(solution)/shard_map/gather | solution.py:77
  120.6 18.8 %while.11 = (s32[]{:T(128)}, f32[1024]{0:T(1024)S(1)}, bf16[8,2048,128]{2,1,0:T(8,128)(2,1)}, bf16[1024,128]{1,0:T(8,128)(2,1)S(1)}, f32[1024]{0:T(1024)S(1)}, /*index=5*/s32[]{:T(128)}, s32[]{:T(128)}) while((s32[]{:T(128)}, f32[1024]{0:T(1024)S(1)}, bf16[8,2048,128]{2,1,0:T(8,128)(2,1)}, bf16[1024,128]{1,0:T(8,128)(2,1)S(1)}, ...), condition=%wide.region_2.3_spmd.clone, body=%wide.region_0.2_spmd.clone.sunk | while | flops 543163392 | bytes 807511 | solution.py:49
  120.6 2.3 %maximum_reduce_fusion.2 = f32[1024]{0:T(1024)S(1)} fusion(bf16[1024,128]{1,0:T(8,128)(2,1)S(1)} %get-tuple-element.115, f32[1024]{0:T(1024)S(1)} %get-tuple-element.116, bf16[8,2048,128]{2,1,0:T(8,128)(2,1)} %get-tuple-element.114, s32[]{:T(128)} %get-tuple-element.105), kind=kOutput, calls=%fused_computation.4.clone.1 | convolution fusion | flops 543161344 | bytes 795136 | tf_op jit(solution)/shard_map/while/body/eval_jaxpr/dot_general | solution.py:44
  123.0 2.3 %maximum_reduce_fusion.2 = f32[1024]{0:T(1024)S(1)} fusion(bf16[1024,128]{1,0:T(8,128)(2,1)S(1)} %get-tuple-element.115, f32[1024]{0:T(1024)S(1)} %get-tuple-element.116, bf16[8,2048,128]{2,1,0:T(8,128)(2,1)} %get-tuple-element.114, s32[]{:T(128)} %get-tuple-element.105), kind=kOutput, calls=%fused_computation.4.clone.1 | convolution fusion | flops 543161344 | bytes 795136 | tf_op jit(solution)/shard_map/while/body/eval_jaxpr/dot_general | solution.py:44
  125.3 2.3 %maximum_reduce_fusion.2 = f32[1024]{0:T(1024)S(1)} fusion(bf16[1024,128]{1,0:T(8,128)(2,1)S(1)} %get-tuple-element.115, f32[1024]{0:T(1024)S(1)} %get-tuple-element.116, bf16[8,2048,128]{2,1,0:T(8,128)(2,1)} %get-tuple-element.114, s32[]{:T(128)} %get-tuple-element.105), kind=kOutput, calls=%fused_computation.4.clone.1 | convolution fusion | flops 543161344 | bytes 795136 | tf_op jit(solution)/shard_map/while/body/eval_jaxpr/dot_general | solution.py:44
  127.7 2.3 %maximum_reduce_fusion.2 = f32[1024]{0:T(1024)S(1)} fusion(bf16[1024,128]{1,0:T(8,128)(2,1)S(1)} %get-tuple-element.115, f32[1024]{0:T(1024)S(1)} %get-tuple-element.116, bf16[8,2048,128]{2,1,0:T(8,128)(2,1)} %get-tuple-element.114, s32[]{:T(128)} %get-tuple-element.105), kind=kOutput, calls=%fused_computation.4.clone.1 | convolution fusion | flops 543161344 | bytes 795136 | tf_op jit(solution)/shard_map/while/body/eval_jaxpr/dot_general | solution.py:44
  130.0 2.3 %maximum_reduce_fusion.2 = f32[1024]{0:T(1024)S(1)} fusion(bf16[1024,128]{1,0:T(8,128)(2,1)S(1)} %get-tuple-element.115, f32[1024]{0:T(1024)S(1)} %get-tuple-element.116, bf16[8,2048,128]{2,1,0:T(8,128)(2,1)} %get-tuple-element.114, s32[]{:T(128)} %get-tuple-element.105), kind=kOutput, calls=%fused_computation.4.clone.1 | convolution fusion | flops 543161344 | bytes 795136 | tf_op jit(solution)/shard_map/while/body/eval_jaxpr/dot_general | solution.py:44
  132.4 2.3 %maximum_reduce_fusion.2 = f32[1024]{0:T(1024)S(1)} fusion(bf16[1024,128]{1,0:T(8,128)(2,1)S(1)} %get-tuple-element.115, f32[1024]{0:T(1024)S(1)} %get-tuple-element.116, bf16[8,2048,128]{2,1,0:T(8,128)(2,1)} %get-tuple-element.114, s32[]{:T(128)} %get-tuple-element.105), kind=kOutput, calls=%fused_computation.4.clone.1 | convolution fusion | flops 543161344 | bytes 795136 | tf_op jit(solution)/shard_map/while/body/eval_jaxpr/dot_general | solution.py:44
  134.7 2.3 %maximum_reduce_fusion.2 = f32[1024]{0:T(1024)S(1)} fusion(bf16[1024,128]{1,0:T(8,128)(2,1)S(1)} %get-tuple-element.115, f32[1024]{0:T(1024)S(1)} %get-tuple-element.116, bf16[8,2048,128]{2,1,0:T(8,128)(2,1)} %get-tuple-element.114, s32[]{:T(128)} %get-tuple-element.105), kind=kOutput, calls=%fused_computation.4.clone.1 | convolution fusion | flops 543161344 | bytes 795136 | tf_op jit(solution)/shard_map/while/body/eval_jaxpr/dot_general | solution.py:44
  137.1 2.3 %maximum_reduce_fusion.2 = f32[1024]{0:T(1024)S(1)} fusion(bf16[1024,128]{1,0:T(8,128)(2,1)S(1)} %get-tuple-element.115, f32[1024]{0:T(1024)S(1)} %get-tuple-element.116, bf16[8,2048,128]{2,1,0:T(8,128)(2,1)} %get-tuple-element.114, s32[]{:T(128)} %get-tuple-element.105), kind=kOutput, calls=%fused_computation.4.clone.1 | convolution fusion | flops 543161344 | bytes 795136 | tf_op jit(solution)/shard_map/while/body/eval_jaxpr/dot_general | solution.py:44
  139.4 0.7 reshape.217
  140.1 3.5 %all-to-all-start = ((f32[16,2,32]{2,1,0:T(2,128)}), f32[16,2,32]{2,1,0:T(2,128)S(1)}, u32[]{:S(2)}, u32[]{:S(2)}) async-start(f32[16,2,32]{2,1,0:T(2,128)} %reshape.217), calls=%async_computation | async-start | bytes 32768 | tf_op jit(solution)/shard_map/all_to_all | solution.py:91
  143.6 0.5 fusion.3
  144.1 0.7 reshape.224
  144.8 6.1 %all-to-all-done = f32[16,2,32]{2,1,0:T(2,128)S(1)} async-done(((f32[16,2,32]{2,1,0:T(2,128)}), f32[16,2,32]{2,1,0:T(2,128)S(1)}, u32[]{:S(2)}, u32[]{:S(2)}) %all-to-all-start) | async-done | bytes 4128 | tf_op jit(solution)/shard_map/all_to_all | solution.py:91
  151.0 3.7 %all_to_all.31 = f32[2,1,512]{2,1,0:T(1,128)S(1)} all-to-all(f32[2,1,512]{2,1,0:T(1,128)S(1)} %reshape.269), channel_id=1, replica_groups=mesh['rows'=16,'feat'=2] {'feat'}, dimensions={0} | all-to-all | bytes 8192 | tf_op jit(solution)/shard_map/all_to_all | solution.py:90
  154.7 3.5 %all-to-all-start.4 = ((f32[16,2,100]{2,1,0:T(2,128)}), f32[16,2,100]{2,1,0:T(2,128)S(1)}, u32[]{:S(2)}, u32[]{:S(2)}) async-start(f32[16,2,100]{2,1,0:T(2,128)} %reshape.224), calls=%async_computation.4 | async-start | bytes 32768 | tf_op jit(solution)/shard_map/all_to_all | solution.py:84
  158.2 0.5 broadcast.322
  158.7 0.7 reduce.15
  159.5 0.5 broadcast_multiply_fusion
  160.0 5.5 %all-to-all-done.4 = f32[16,2,100]{2,1,0:T(2,128)S(1)} async-done(((f32[16,2,100]{2,1,0:T(2,128)}), f32[16,2,100]{2,1,0:T(2,128)S(1)}, u32[]{:S(2)}, u32[]{:S(2)}) %all-to-all-start.4) | async-done | bytes 12832 | tf_op jit(solution)/shard_map/all_to_all | solution.py:84
  165.5 3.7 %all_to_all.32 = f32[16,2,100]{2,0,1:T(8,128)S(1)} all-to-all(f32[16,2,100]{2,0,1:T(8,128)S(1)} %copy.55), channel_id=1, replica_groups=mesh['rows'=16,'feat'=2] {'feat'}, dimensions={1} | all-to-all | bytes 25600 | tf_op jit(solution)/shard_map/all_to_all | solution.py:83
  169.2 19.0 %gather_fusion.2 = f32[3200]{0:T(1024)S(1)} fusion(f32[32,100]{1,0:T(8,128)S(1)} %bitcast.33, s32[3200]{0:T(1024)S(1)} %get-tuple-element.58), kind=kCustom, calls=%fused_computation.2 | custom fusion | bytes 51200 | tf_op jit(solution)/shard_map/gather | solution.py:99
  188.2 0.7 reshape.226
  (70 shorter events, 2.3 us)
Async XLA Ops:
  4.1 41.0 %collective-permute-start = (bf16[64,128]{1,0:T(8,128)(2,1)}, bf16[64,128]{1,0:T(8,128)(2,1)}, u32[]{:S(2)}, u32[]{:S(2)}) collective-permute-start(bf16[64,128]{1,0:T(8,128)(2,1)} %copy.45), channel_id=1, source_target_pairs={{0,2},{2,4},{4,6},{6,8},{8,10},{10,12},{12,14},{14,16},{16,18},{18... | collective-permute-start | bytes 49160 | tf_op jit(solution)/shard_map/ppermute | solution.py:16
  6.9 40.0 %collective-permute-start.1 = (bf16[64,128]{1,0:T(8,128)(2,1)}, bf16[64,128]{1,0:T(8,128)(2,1)}, u32[]{:S(2)}, u32[]{:S(2)}) collective-permute-start(bf16[64,128]{1,0:T(8,128)(2,1)} %copy.45), channel_id=1, source_target_pairs={{0,30},{2,0},{4,2},{6,4},{8,6},{10,8},{12,10},{14,12},{16,14},{18,... | collective-permute-start | bytes 49160 | tf_op jit(solution)/shard_map/ppermute | solution.py:21
  13.5 11.0 %copy-start.4 = (s32[2]{0:T(128)S(1)}, s32[2]{0:T(128)}, u32[]{:S(2)}) copy-start(s32[2]{0:T(128)} %constant.167) | copy-start | bytes 28
  13.5 11.1 %copy-start.3 = (s32[2]{0:T(128)S(1)}, s32[2]{0:T(128)}, u32[]{:S(2)}) copy-start(s32[2]{0:T(128)} %constant.164) | copy-start | bytes 28
  25.3 18.5 %copy-start.1 = (s32[1024]{0:T(1024)S(1)}, s32[1024]{0:T(1024)}, u32[]{:S(2)}) copy-start(s32[1024]{0:T(1024)} %param.9) | copy-start | bytes 12292
  40.3 19.6 %all-to-all-start.2 = ((s32[16,2,200]{2,1,0:T(2,128)}), s32[16,2,200]{2,1,0:T(2,128)S(1)}, u32[]{:S(2)}, u32[]{:S(2)}) async-start(s32[16,2,200]{2,1,0:T(2,128)} %reshape.222), calls=%async_computation.2 | async-start | bytes 65536 | tf_op jit(solution)/shard_map/all_to_all | solution.py:63
  45.1 7.7 %collective-permute-start.2 = (bf16[64,128]{1,0:T(8,128)(2,1)}, bf16[64,128]{1,0:T(8,128)(2,1)}, u32[]{:S(2)}, u32[]{:S(2)}) collective-permute-start(bf16[64,128]{1,0:T(8,128)(2,1)} %collective-permute-done), channel_id=1, source_target_pairs={{0,2},{2,4},{4,6},{6,8},{8,10},{10,12},{12,14},{14,16},{16,18},{18... | collective-permute-start | bytes 49160 | tf_op jit(solution)/shard_map/ppermute | solution.py:16
  47.0 5.8 %collective-permute-start.3 = (bf16[64,128]{1,0:T(8,128)(2,1)}, bf16[64,128]{1,0:T(8,128)(2,1)}, u32[]{:S(2)}, u32[]{:S(2)}) collective-permute-start(bf16[64,128]{1,0:T(8,128)(2,1)} %collective-permute-done.1), channel_id=1, source_target_pairs={{0,30},{2,0},{4,2},{6,4},{8,6},{10,8},{12,10},{14,12},{16,14},{18,... | collective-permute-start | bytes 49160 | tf_op jit(solution)/shard_map/ppermute | solution.py:21
  52.8 24.1 %collective-permute-start.4 = (bf16[64,128]{1,0:T(8,128)(2,1)}, bf16[64,128]{1,0:T(8,128)(2,1)}, u32[]{:S(2)}, u32[]{:S(2)}) collective-permute-start(bf16[64,128]{1,0:T(8,128)(2,1)} %collective-permute-done.2), channel_id=1, source_target_pairs={{0,2},{2,4},{4,6},{6,8},{8,10},{10,12},{12,14},{14,16},{16,18},{18... | collective-permute-start | bytes 49160 | tf_op jit(solution)/shard_map/ppermute | solution.py:16
  52.8 24.2 %collective-permute-start.5 = (bf16[64,128]{1,0:T(8,128)(2,1)}, bf16[64,128]{1,0:T(8,128)(2,1)}, u32[]{:S(2)}, u32[]{:S(2)}) collective-permute-start(bf16[64,128]{1,0:T(8,128)(2,1)} %collective-permute-done.3), channel_id=1, source_target_pairs={{0,30},{2,0},{4,2},{6,4},{8,6},{10,8},{12,10},{14,12},{16,14},{18,... | collective-permute-start | bytes 49160 | tf_op jit(solution)/shard_map/ppermute | solution.py:21
  76.9 7.6 %collective-permute-start.6 = (bf16[64,128]{1,0:T(8,128)(2,1)}, bf16[64,128]{1,0:T(8,128)(2,1)S(1)}, u32[]{:S(2)}, u32[]{:S(2)}) collective-permute-start(bf16[64,128]{1,0:T(8,128)(2,1)} %collective-permute-done.4), channel_id=1, source_target_pairs={{0,2},{2,4},{4,6},{6,8},{8,10},{10,12},{12,14},{14,16},{16,18},{18... | collective-permute-start | bytes 49160 | tf_op jit(solution)/shard_map/ppermute | solution.py:16
  77.0 7.5 %collective-permute-start.7 = (bf16[64,128]{1,0:T(8,128)(2,1)}, bf16[64,128]{1,0:T(8,128)(2,1)S(1)}, u32[]{:S(2)}, u32[]{:S(2)}) collective-permute-start(bf16[64,128]{1,0:T(8,128)(2,1)} %collective-permute-done.5), channel_id=1, source_target_pairs={{0,30},{2,0},{4,2},{6,4},{8,6},{10,8},{12,10},{14,12},{16,14},{18,... | collective-permute-start | bytes 49160 | tf_op jit(solution)/shard_map/ppermute | solution.py:21
  84.5 7.3 %collective-permute-start.8 = (bf16[64,128]{1,0:T(8,128)(2,1)S(1)}, bf16[64,128]{1,0:T(8,128)(2,1)S(1)}, u32[]{:S(2)}, u32[]{:S(2)}) collective-permute-start(bf16[64,128]{1,0:T(8,128)(2,1)S(1)} %collective-permute-done.6), channel_id=1, source_target_pairs={{0,2},{2,4},{4,6},{6,8},{8,10},{10,12},{12,14},{14,16},{16,18},{18... | collective-permute-start | bytes 49160 | tf_op jit(solution)/shard_map/ppermute | solution.py:16
  84.5 7.3 %collective-permute-start.9 = (bf16[64,128]{1,0:T(8,128)(2,1)S(1)}, bf16[64,128]{1,0:T(8,128)(2,1)S(1)}, u32[]{:S(2)}, u32[]{:S(2)}) collective-permute-start(bf16[64,128]{1,0:T(8,128)(2,1)S(1)} %collective-permute-done.7), channel_id=1, source_target_pairs={{0,30},{2,0},{4,2},{6,4},{8,6},{10,8},{12,10},{14,12},{16,14},{18,... | collective-permute-start | bytes 49160 | tf_op jit(solution)/shard_map/ppermute | solution.py:21
  91.9 7.3 %collective-permute-start.10 = (bf16[64,128]{1,0:T(8,128)(2,1)S(1)}, bf16[64,128]{1,0:T(8,128)(2,1)S(1)}, u32[]{:S(2)}, u32[]{:S(2)}) collective-permute-start(bf16[64,128]{1,0:T(8,128)(2,1)S(1)} %collective-permute-done.8), channel_id=1, source_target_pairs={{0,2},{2,4},{4,6},{6,8},{8,10},{10,12},{12,14},{14,16},{16,18},{18... | collective-permute-start | bytes 49160 | tf_op jit(solution)/shard_map/ppermute | solution.py:16
  91.9 7.3 %collective-permute-start.11 = (bf16[64,128]{1,0:T(8,128)(2,1)S(1)}, bf16[64,128]{1,0:T(8,128)(2,1)S(1)}, u32[]{:S(2)}, u32[]{:S(2)}) collective-permute-start(bf16[64,128]{1,0:T(8,128)(2,1)S(1)} %collective-permute-done.9), channel_id=1, source_target_pairs={{0,30},{2,0},{4,2},{6,4},{8,6},{10,8},{12,10},{14,12},{16,14},{18,... | collective-permute-start | bytes 49160 | tf_op jit(solution)/shard_map/ppermute | solution.py:21
  99.2 7.3 %collective-permute-start.12 = (bf16[64,128]{1,0:T(8,128)(2,1)S(1)}, bf16[64,128]{1,0:T(8,128)(2,1)S(1)}, u32[]{:S(2)}, u32[]{:S(2)}) collective-permute-start(bf16[64,128]{1,0:T(8,128)(2,1)S(1)} %collective-permute-done.10), channel_id=1, source_target_pairs={{0,2},{2,4},{4,6},{6,8},{8,10},{10,12},{12,14},{14,16},{16,18},{18... | collective-permute-start | bytes 49160 | tf_op jit(solution)/shard_map/ppermute | solution.py:16
  99.2 7.3 %collective-permute-start.13 = (bf16[64,128]{1,0:T(8,128)(2,1)S(1)}, bf16[64,128]{1,0:T(8,128)(2,1)S(1)}, u32[]{:S(2)}, u32[]{:S(2)}) collective-permute-start(bf16[64,128]{1,0:T(8,128)(2,1)S(1)} %collective-permute-done.11), channel_id=1, source_target_pairs={{0,30},{2,0},{4,2},{6,4},{8,6},{10,8},{12,10},{14,12},{16,14},{18,... | collective-permute-start | bytes 49160 | tf_op jit(solution)/shard_map/ppermute | solution.py:21
  106.5 7.3 %collective-permute-start.14 = (bf16[64,128]{1,0:T(8,128)(2,1)S(1)}, bf16[64,128]{1,0:T(8,128)(2,1)S(1)}, u32[]{:S(2)}, u32[]{:S(2)}) collective-permute-start(bf16[64,128]{1,0:T(8,128)(2,1)S(1)} %collective-permute-done.12), channel_id=1, source_target_pairs={{0,2},{2,4},{4,6},{6,8},{8,10},{10,12},{12,14},{14,16},{16,18},{18... | collective-permute-start | bytes 49160 | tf_op jit(solution)/shard_map/ppermute | solution.py:16
  113.9 6.7 %copy-start = (f32[1024]{0:T(1024)S(1)}, f32[1024]{0:T(1024)}, u32[]{:S(2)}) copy-start(f32[1024]{0:T(1024)} %custom-call.2) | copy-start | bytes 12292
  113.9 6.7 %copy-start.2 = (f32[1024]{0:T(1024)S(1)}, f32[1024]{0:T(1024)}, u32[]{:S(2)}) copy-start(f32[1024]{0:T(1024)} %convert_multiply_fusion.1) | copy-start | bytes 12292
  140.1 10.8 %all-to-all-start = ((f32[16,2,32]{2,1,0:T(2,128)}), f32[16,2,32]{2,1,0:T(2,128)S(1)}, u32[]{:S(2)}, u32[]{:S(2)}) async-start(f32[16,2,32]{2,1,0:T(2,128)} %reshape.217), calls=%async_computation | async-start | bytes 32768 | tf_op jit(solution)/shard_map/all_to_all | solution.py:91
  154.7 10.8 %all-to-all-start.4 = ((f32[16,2,100]{2,1,0:T(2,128)}), f32[16,2,100]{2,1,0:T(2,128)S(1)}, u32[]{:S(2)}, u32[]{:S(2)}) async-start(f32[16,2,100]{2,1,0:T(2,128)} %reshape.224), calls=%async_computation.4 | async-start | bytes 32768 | tf_op jit(solution)/shard_map/all_to_all | solution.py:84
